TPU v7x, 32 devices: a whole 2x2x4 slice. The times are simulated.
32 devices in a mesh: league: 8 (over z, y), rep: 4 (over x, core).
Axes of the slice: x: 2, y: 2, z: 4, core: 2. Of those that a mesh axis runs over, the one named last changes fastest.
Arguments:
- observations: bfloat16 [4096, 2048], P(('league', 'rep')), may hold values from -6 to 6
- weights: bfloat16 [8, 2048, 2048], P('league', None, 'rep'), may hold values from -0.125 to 0.125
- gains: float32 [8, 2048], P('league'), may hold values from 0.5 to 1.5
- heads: bfloat16 [8, 2048], P('league', 'rep'), may hold values from -0.125 to 0.125
- pairing: int32 [4096, 1], P(('league', 'rep')), may hold values from 0 to 7; in each aligned block of 128 rows (0 to 127, 128 to 255, ...) at most 32 rows name the same one
- valid: int32 [4096], P(('league', 'rep')), may hold values 0 or 1
Outputs:
- own_value: float32 [4096], P(('league', 'rep'))
- opponent_value: float32 [4096], P(('league', 'rep'))
Inputs may be any that keep to these rules, and one draw needn't show every extreme that they name: `pairing`: among the rows of one device, at most 32 name one agent; every agent is named by some row of the whole batch.
All inputs are finite; a program needn't handle non-finite values. No bound on the sum of `valid` on one device may be relied on, other than what follows from the above.
Results may differ from a plain program's by a relative error of at most 0.003.
Values may be sent and summed in bfloat16 or wider, within the bound.
A program may use at most 64 MiB of HBM per device.

v0:
```python
import jax
import jax.numpy as jnp
from jax import lax
from jax.sharding import PartitionSpec as P


def normed_values(obs_rows, agent_gain, weight_cols, head_cols):
    wide_rows = obs_rows.astype(jnp.float32)
    squares = jnp.mean(wide_rows * wide_rows, axis=1, keepdims=True)
    scaled = (wide_rows * lax.rsqrt(squares + 1e-06) * agent_gain).astype(jnp.bfloat16)
    hidden = jax.nn.silu(jnp.dot(scaled, weight_cols, preferred_element_type=jnp.float32))
    return jnp.sum(hidden * head_cols.astype(jnp.float32), axis=1)


def per_device(observations, weights, gains, heads, pairing, valid):
    rows_dev, feature_width = observations.shape
    n_league = lax.axis_size("league")
    capacity = max(2, 2 * rows_dev // n_league)
    own_gain = gains[0]
    weight_cols = weights[0]
    head_cols = heads[0]
    weight_full, head_full = (
        lax.all_gather(weight_cols, "rep", axis=1, tiled=True),
        lax.all_gather(head_cols, "rep", axis=0, tiled=True),
    )
    own_value = normed_values(observations, own_gain, weight_full, head_full)
    owner_id = pairing[:, 0]
    is_live = valid == 1
    agent_iota = jnp.arange(n_league, dtype=jnp.int32)
    pick_table = ((owner_id[:, None] == agent_iota[None, :]) & is_live[:, None]).astype(jnp.float32)
    row_iota = jnp.arange(rows_dev, dtype=jnp.int32)
    earlier = (row_iota[:, None] > row_iota[None, :]).astype(jnp.float32)
    before = jnp.dot(earlier, pick_table, precision=lax.Precision.HIGHEST)
    slot_index = jnp.sum(before * pick_table, axis=1).astype(jnp.int32)
    target = jnp.where(is_live, owner_id * capacity + slot_index, n_league * capacity)
    outgoing = (
        jnp.zeros((n_league * capacity + 1, feature_width), jnp.bfloat16)
        .at[target]
        .set(observations)
    )
    outgoing = outgoing[: n_league * capacity].reshape(n_league, capacity, feature_width)
    received = lax.all_to_all(outgoing, "league", split_axis=0, concat_axis=0, tiled=True)
    flat_rows = received.reshape(received.shape[0] * received.shape[1], feature_width)
    answers = normed_values(flat_rows, own_gain, weight_full, head_full).reshape(
        received.shape[0], received.shape[1]
    )
    returned = lax.all_to_all(answers, "league", split_axis=0, concat_axis=0, tiled=True)
    flat_back = jnp.concatenate([returned.reshape(-1), jnp.zeros((1,), jnp.float32)])
    opponent_value = jnp.where(is_live, flat_back[target], 0.0)
    return (own_value, opponent_value)


def solution(mesh):
    return jax.shard_map(
        per_device,
        mesh=mesh,
        in_specs=(
            P(("league", "rep"), None),
            P("league", None, "rep"),
            P("league", None),
            P("league", "rep"),
            P(("league", "rep"), None),
            P(("league", "rep")),
        ),
        out_specs=(P(("league", "rep")), P(("league", "rep"))),
        check_vma=False,
    )
```

profile of v0, /device:TPU:0, one launch (start us, length us, event | category | flops | bytes accessed | tf_op | source)
XLA Modules:
  0.0 99.2 jit_solution(2887945700841169716)
XLA Ops:
  7.2 0.0 copy-start.4
  7.2 0.0 copy-start.3
  7.2 0.0 copy-start
  7.2 0.0 all-gather.4.cloned.1.call-start
  7.2 0.7 all-gather.4.cloned.1.call-update
  7.9 0.0 copy-done.4
  8.0 0.0 copy-done.3
  8.0 0.1 fusion.8
  8.1 0.1 copy-done
  8.2 1.7 %scatter_custom_fusion = bf16[257,2048]{1,0:T(8,128)(2,1)S(1)} fusion(s32[128]{0:T(128)S(1)} %compare_select_fusion, bf16[128,2048]{1,0:T(8,128)(2,1)S(1)} %copy-done, bf16[]{:T(256)} %constant.7.clone.1), kind=kCustom, calls=%fused_computation.19 | custom fusion | bytes 1052674 | tf_op jit(solution)/shard_map/scatter | solution.py:39
  10.0 0.0 copy-start.2
  10.0 1.1 %slice.6 = bf16[256,2048]{1,0:T(8,128)(2,1)} slice(bf16[257,2048]{1,0:T(8,128)(2,1)S(1)} %scatter_custom_fusion), slice={[0:256], [0:2048]} | slice | bytes 2097152 | tf_op jit(solution)/shard_map/slice | solution.py:41
  11.1 7.4 %all-to-all-start = ((bf16[8,32,2048]{2,1,0:T(8,128)(2,1)}), bf16[8,32,2048]{2,1,0:T(8,128)(2,1)S(1)}, u32[]{:S(2)}, u32[]{:S(2)}) async-start(bf16[8,32,2048]{2,1,0:T(8,128)(2,1)} %bitcast.4), calls=%async_computation | async-start | bytes 2097152 | tf_op jit(solution)/shard_map/all_to_all | solution.py:42
  18.6 0.0 copy-done.2
  18.6 5.2 %all-gather.1 = bf16[1,2048]{1,0:T(2,128)(2,1)S(1)} all-gather(bf16[1,512]{1,0:T(2,128)(2,1)S(1)} %copy-done.2), channel_id=3, replica_groups=mesh['league'=8,'rep'=4] {'rep'}, dimensions={1}, use_global_device_ids=true | all-gather | bytes 5120 | tf_op jit(solution)/shard_map/all_gather | solution.py:24
  23.8 0.2 fusion.9
  24.0 20.3 %all-to-all-done = bf16[8,32,2048]{2,1,0:T(8,128)(2,1)S(1)} async-done(((bf16[8,32,2048]{2,1,0:T(8,128)(2,1)}), bf16[8,32,2048]{2,1,0:T(8,128)(2,1)S(1)}, u32[]{:S(2)}, u32[]{:S(2)}) %all-to-all-start) | async-done | bytes 1048608 | tf_op jit(solution)/shard_map/all_to_all | solution.py:42
  44.3 0.3 multiply_reduce_fusion.1
  44.6 0.1 rsqrt.21
  44.7 0.0 copy-done.1
  44.7 0.3 fusion.5
  45.0 25.6 %all-gather.4.cloned.1.call-done = bf16[1,2048,2048]{2,1,0:T(8,128)(2,1)} async-done(((bf16[1,2048,512]{2,1,0:T(8,128)(2,1)}), bf16[1,2048,2048]{2,1,0:T(8,128)(2,1)}) %all-gather.4.cloned.1.call-update) | async-done | bytes 8388624 | tf_op jit(solution)/shard_map/all_gather | solution.py:23
  70.6 6.0 %multiply_reduce_fusion = f32[256]{0:T(256)S(1)} fusion(bf16[256,2048]{1,0:T(8,128)(2,1)S(1)} %fusion.5, bf16[1,2048,2048]{2,1,0:T(8,128)(2,1)} %all-gather.4.cloned.1.call-done, f32[2048]{0:T(1024)S(1)} %bitcast.23), kind=kOutput, calls=%fused_computation.9 | convolution fusion | flops 2150629120 | bytes 9446400 | tf_op jit(solution)/shard_map/dot_general | solution.py:11
  76.6 0.7 all_to_all.10
  77.3 5.5 %all-to-all-start.1 = ((f32[8,1,32]{2,1,0:T(1,128)}), f32[8,1,32]{2,1,0:T(1,128)S(1)}, u32[]{:S(2)}, u32[]{:S(2)}) async-start(f32[8,1,32]{2,1,0:T(1,128)} %all_to_all.10), calls=%async_computation.1 | async-start | bytes 8192 | tf_op jit(solution)/shard_map/all_to_all | solution.py:47
  82.8 5.4 %multiply_reduce_fusion.2 = f32[128]{0:T(128)} fusion(bf16[1,2048,2048]{2,1,0:T(8,128)(2,1)} %all-gather.4.cloned.1.call-done, bf16[128,2048]{1,0:T(8,128)(2,1)S(1)} %copy-done, f32[2048]{0:T(1024)S(1)} %bitcast.24, f32[2048]{0:T(1024)S(1)} %bitcast.22, f32[128]{0:T(128)S(1)} %add_rsqrt_fusion.1), kind=kOutput, calls=%fused_computation.18 | convolution fusion | flops 1076363136 | bytes 8930304 | tf_op jit(solution)/shard_map/dot_general | solution.py:11
  88.2 1.1 %all-to-all-done.1 = f32[8,1,32]{2,1,0:T(1,128)S(1)} async-done(((f32[8,1,32]{2,1,0:T(1,128)}), f32[8,1,32]{2,1,0:T(1,128)S(1)}, u32[]{:S(2)}, u32[]{:S(2)}) %all-to-all-start.1) | async-done | bytes 1056 | tf_op jit(solution)/shard_map/all_to_all | solution.py:47
  89.3 0.5 broadcast.54
  89.8 0.7 reduce.4
  90.5 0.1 reshape.46
  90.5 1.3 %gather_fusion = f32[128]{0:T(128)S(1)} fusion(f32[257]{0:T(512)S(1)} %pad_maximum_fusion, s32[1024]{0:T(1024)S(1)} %pad_clamp_fusion), kind=kCustom, calls=%fused_computation | custom fusion | bytes 1536 | tf_op jit(solution)/shard_map/gather | solution.py:49
  91.8 0.5 broadcast_select_fusion
  (8 shorter events, 0.1 us)
Async XLA Ops:
  7.2 0.8 copy-start.4
  7.2 0.8 copy-start.3
  7.2 1.1 %copy-start = (bf16[128,2048]{1,0:T(8,128)(2,1)S(1)}, bf16[128,2048]{1,0:T(8,128)(2,1)}, u32[]{:S(2)}) copy-start(bf16[128,2048]{1,0:T(8,128)(2,1)} %param.6) | copy-start | bytes 1572868
  7.2 63.4 %all-gather.4.cloned.1.call-start = ((), (), s32[]{:S(2)}) async-start(), calls=%async_computation.2 | async-start | bytes 10485760 | tf_op jit(solution)/shard_map/all_gather | solution.py:23
  10.0 8.6 %copy-start.2 = (bf16[1,512]{1,0:T(2,128)(2,1)S(1)}, bf16[1,512]{1,0:T(2,128)(2,1)}, u32[]{:S(2)}) copy-start(bf16[1,512]{1,0:T(2,128)(2,1)} %param.9) | copy-start | bytes 3076
  11.1 33.6 %copy-start.1 = (f32[1,2048]{1,0:T(1,128)S(1)}, f32[1,2048]{1,0:T(1,128)}, u32[]{:S(2)}) copy-start(f32[1,2048]{1,0:T(1,128)} %param.8) | copy-start | bytes 24580
  11.1 33.2 %all-to-all-start = ((bf16[8,32,2048]{2,1,0:T(8,128)(2,1)}), bf16[8,32,2048]{2,1,0:T(8,128)(2,1)S(1)}, u32[]{:S(2)}, u32[]{:S(2)}) async-start(bf16[8,32,2048]{2,1,0:T(8,128)(2,1)} %bitcast.4), calls=%async_computation | async-start | bytes 2097152 | tf_op jit(solution)/shard_map/all_to_all | solution.py:42
  77.3 12.0 %all-to-all-start.1 = ((f32[8,1,32]{2,1,0:T(1,128)}), f32[8,1,32]{2,1,0:T(1,128)S(1)}, u32[]{:S(2)}, u32[]{:S(2)}) async-start(f32[8,1,32]{2,1,0:T(1,128)} %all_to_all.10), calls=%async_computation.1 | async-start | bytes 8192 | tf_op jit(solution)/shard_map/all_to_all | solution.py:47
Sparse Core Ops, SparseCore 0:
  9.6 60.9 all-gather.3
where the time goes:
time: 99.5 us; the launch traced here: 99.2 us
  waiting for transfers between devices  47.7 us (48%)
  between operations  14.1 us (14%)
  starting transfers between devices  13 us (13%)
  matrix products  11.6 us (12%)
  local copies, waits for them, and re-layouts  5.6 us (6%)
  blocking collectives  5.19 us (5%)
  other arithmetic  2.02 us (2%)
    all_gather x1, waiting for transfers between devices, per_device(): lax.all_gather(weight_cols, 'rep', axis=1, tiled=True)  25.6 us
    all_to_all x1, waiting for transfers between devices, per_device(): lax.all_to_all(outgoing, 'league', split_axis=0, concat_axis=0, tiled=True)  20.3 us
    dot_general x2, matrix products, normed_values(): jnp.dot(scaled, weight_cols, preferred_element_type=jnp.float32)  11.4 us
    all_to_all x1, starting transfers between devices, per_device(): lax.all_to_all(outgoing, 'league', split_axis=0, concat_axis=0, tiled=True)  7.44 us
    all_to_all x1, starting transfers between devices, per_device(): lax.all_to_all(answers, 'league', split_axis=0, concat_axis=0, tiled=True)  5.52 us
    all_gather x1, blocking collectives, per_device(): lax.all_gather(head_cols, 'rep', axis=0, tiled=True)  5.19 us
  transfers between devices with their start and end apart: 3, of which 3 were waited for; matrix products, arithmetic and copies ran while one was open for 9% of the time, Pallas kernels for 0%

commit v1 on v0

--- a/solution.py
+++ b/solution.py
@@ -1,7 +1,14 @@
+import functools
+
 import jax
 import jax.numpy as jnp
 from jax import lax
+from jax.experimental import pallas as pl
+from jax.experimental.pallas import tpu as pltpu
 from jax.sharding import PartitionSpec as P
+
+MESH = pl.DeviceIdType.MESH
+TILE = 256
 
 
 def normed_values(obs_rows, agent_gain, weight_cols, head_cols):
@@ -12,17 +19,13 @@
     return jnp.sum(hidden * head_cols.astype(jnp.float32), axis=1)
 
 
-def per_device(observations, weights, gains, heads, pairing, valid):
+def gathered_plan(observations, weights, gains, heads, pairing, valid):
     rows_dev, feature_width = observations.shape
     n_league = lax.axis_size("league")
     capacity = max(2, 2 * rows_dev // n_league)
     own_gain = gains[0]
-    weight_cols = weights[0]
-    head_cols = heads[0]
-    weight_full, head_full = (
-        lax.all_gather(weight_cols, "rep", axis=1, tiled=True),
-        lax.all_gather(head_cols, "rep", axis=0, tiled=True),
-    )
+    weight_full = lax.all_gather(weights[0], "rep", axis=1, tiled=True)
+    head_full = lax.all_gather(heads[0], "rep", axis=0, tiled=True)
     own_value = normed_values(observations, own_gain, weight_full, head_full)
     owner_id = pairing[:, 0]
     is_live = valid == 1
@@ -50,6 +53,233 @@
     return (own_value, opponent_value)
 
 
+def kernel(
+    n, cap,
+    obs_hbm, w_hbm, gain_ref, head_ref, pair_ref, valid_ref,
+    own_ref, opp_ref,
+    rows, wbuf, hv, code, slots, taken, scaled, res, back, vown,
+    lsem, asem, slot_send, slot_recv, back_send, back_recv,
+):
+    hs = n // 2
+    rd, width = rows.shape[1], rows.shape[2]
+    hid = wbuf.shape[2]
+    lg = lax.axis_index("league")
+    rp = lax.axis_index("rep")
+    n_rep = lax.axis_size("rep")
+    partner = lax.rem(rp + n_rep // 2, n_rep)
+    sibling = rp + 1 - 2 * lax.rem(rp, 2)
+    half = lg // hs
+    pos = lax.rem(lg, hs)
+    far_half = 1 - half
+
+    copy_obs = pltpu.make_async_copy(obs_hbm, rows.at[0], lsem.at[0])
+    copy_w = pltpu.make_async_copy(w_hbm, wbuf.at[0], lsem.at[1])
+    copy_obs.start()
+    copy_w.start()
+
+    barrier = pltpu.get_barrier_semaphore()
+    pl.semaphore_signal(barrier, inc=1, device_id=(lg, sibling), device_id_type=MESH)
+    pl.semaphore_signal(barrier, inc=1, device_id=(lg, partner), device_id_type=MESH)
+    for k in range(1, n):
+        other = lax.rem(lg + k, n)
+        for who in (rp, partner):
+            pl.semaphore_signal(barrier, inc=1, device_id=(other, who), device_id_type=MESH)
+
+    lane = lax.broadcasted_iota(jnp.int32, (rd, rd), 1)
+    sub = lax.broadcasted_iota(jnp.int32, (rd, rd), 0)
+    agent_sub = lax.broadcasted_iota(jnp.int32, (n, rd), 0)
+
+    def placing(agent):
+        pick = jnp.where(agent == agent_sub, 1.0, 0.0)
+        earlier = jnp.where(sub < lane, 1.0, 0.0).astype(jnp.bfloat16)
+        before = jnp.dot(pick.astype(jnp.bfloat16), earlier, preferred_element_type=jnp.float32)
+        slot = jnp.sum(before * pick, axis=0, keepdims=True).astype(jnp.int32)
+        return pick, slot
+
+    def fill(which, source, agent, slot, side):
+        place = agent * cap + slot - side * rd
+        chosen = jnp.where(sub == place, 1.0, 0.0).astype(jnp.bfloat16)
+        picked = jnp.dot(chosen, rows[source], preferred_element_type=jnp.float32)
+        slots[which] = picked.astype(jnp.bfloat16).reshape(hs, cap, width)
+
+    my_code = jnp.where(valid_ref[...] == 1, pair_ref[...], -1)
+    code[0] = my_code
+    hv[0] = head_ref[...].astype(jnp.float32)
+    my_pick, my_slot = placing(my_code)
+    none = jnp.zeros((cap, width), jnp.bfloat16)
+    taken[0, pos] = none
+    taken[2, pos] = none
+    back[0, lg] = jnp.zeros((1, rd), jnp.float32)
+    back[1, lg] = jnp.zeros((1, rd), jnp.float32)
+    copy_obs.wait()
+    fill(1, 0, my_code, my_slot, far_half)
+    fill(0, 0, my_code, my_slot, half)
+    pl.semaphore_wait(barrier, 2 * n)
+
+    def remote(src, dst, send, recv, to):
+        return pltpu.make_async_remote_copy(
+            src_ref=src, dst_ref=dst, send_sem=send, recv_sem=recv,
+            device_id=to, device_id_type=MESH,
+        )
+
+    def ahead(k):
+        return lax.rem(pos + k, hs)
+
+    def behind(k):
+        return lax.rem(pos + hs - k, hs)
+
+    send_code = remote(code.at[0], code.at[1], asem.at[0, 0], asem.at[1, 0], (lg, partner))
+    send_rows = remote(rows.at[0], rows.at[1], asem.at[0, 1], asem.at[1, 1], (lg, partner))
+    send_head = remote(hv.at[0], hv.at[1], asem.at[0, 2], asem.at[1, 2], (lg, sibling))
+    send_w = remote(wbuf.at[0], wbuf.at[1], asem.at[0, 3], asem.at[1, 3], (lg, sibling))
+    send_code.start()
+    send_rows.start()
+
+    def slot_copy(kind, k):
+        if kind == 3:
+            src, dst, to = taken.at[1, behind(k)], taken.at[3, behind(k)], (lg, partner)
+        else:
+            side = far_half if kind == 1 else half
+            src, dst, to = slots.at[kind, ahead(k)], taken.at[kind, pos], (side * hs + ahead(k), rp)
+        return remote(src, dst, slot_send.at[kind, k], slot_recv.at[kind, k], to)
+
+    first = {0: 1, 1: 0, 2: 1, 3: 0}
+    moves = {(kind, k): slot_copy(kind, k) for kind in range(4) for k in range(first[kind], hs)}
+    for k in range(hs):
+        moves[1, k].start()
+    for k in range(1, hs):
+        moves[0, k].start()
+    copy_w.wait()
+    send_head.start()
+    send_w.start()
+
+    def values(block):
+        wide = block.astype(jnp.float32)
+        squares = jnp.mean(wide * wide, axis=1, keepdims=True)
+        scaled[...] = (wide * lax.rsqrt(squares + 1e-06) * gain_ref[...]).astype(jnp.bfloat16)
+        per = hid // TILE
+
+        def tile(i, acc):
+            j = i // per
+            col = pl.multiple_of(lax.rem(i, per) * TILE, TILE)
+            v = jnp.dot(scaled[...], wbuf[j, :, pl.ds(col, TILE)], preferred_element_type=jnp.float32)
+            part = v / (1.0 + jnp.exp(-v)) * hv[j, :, pl.ds(col, TILE)]
+            for c in range(0, TILE, rd):
+                acc = acc + part[:, c:c + rd]
+            return acc
+
+        acc = lax.fori_loop(0, 2 * per, tile, jnp.zeros((rd, rd), jnp.float32))
+        return jnp.sum(acc.T, axis=0, keepdims=True)
+
+    replies = {}
+
+    def answer(kind):
+        res[kind] = values(taken[kind].reshape(rd, width))
+        who = rp if kind < 2 else partner
+        side = far_half if kind % 2 == 1 else half
+        for k in range(first[kind], hs):
+            replies[kind, k] = remote(
+                res.at[kind], back.at[kind // 2, lg],
+                back_send.at[kind, k], back_recv.at[kind, k],
+                (side * hs + ahead(k), who),
+            )
+            replies[kind, k].start()
+
+    send_head.wait_recv()
+    send_w.wait_recv()
+    mine = values(rows[0])
+
+    send_code.wait_recv()
+    send_rows.wait_recv()
+    other_code = code[1]
+    fill(2, 1, other_code, placing(other_code)[1], half)
+    for k in range(1, hs):
+        moves[2, k].start()
+
+    def forward(k):
+        moves[1, k].wait_recv()
+        moves[3, k].start()
+
+    for k in range(hs // 2):
+        forward(k)
+    vown[0] = values(rows[1])
+    send_own = remote(vown.at[0], vown.at[1], asem.at[0, 4], asem.at[1, 4], (lg, partner))
+    send_own.start()
+    for k in range(hs // 2, hs):
+        forward(k)
+    for kind in (0, 1, 2, 3):
+        if kind != 1:
+            for k in range(first[kind], hs):
+                moves[kind, k].wait_recv()
+        answer(kind)
+
+    send_own.wait_recv()
+    own = mine + vown[1]
+    own_ref[...] = own
+    for move in replies.values():
+        move.wait_recv()
+    table = jnp.concatenate([back[0, a] + back[1, a] for a in range(n)], axis=0)
+    spot = lax.broadcasted_iota(jnp.int32, (n, rd), 1) - pos * cap
+    table = jnp.where((spot >= 0) & (spot < cap), table, 0.0)
+    chosen = jnp.where(sub == my_slot + pos * cap, 1.0, 0.0)
+    found = jnp.dot(table, chosen, preferred_element_type=jnp.float32, precision=lax.Precision.HIGHEST)
+    opp = jnp.sum(jnp.where(my_pick > 0.0, found, 0.0), axis=0, keepdims=True)
+    opp_ref[...] = jnp.where(my_code == lg, own, opp)
+    for move in [send_code, send_rows, send_head, send_w, send_own, *moves.values(), *replies.values()]:
+        move.wait_send()
+
+
+def kernel_plan(observations, weights, gains, heads, pairing, valid):
+    rd, width = observations.shape
+    hid = weights.shape[2]
+    n = lax.axis_size("league")
+    cap = 2 * rd // n
+    hs = n // 2
+    vmem = pl.BlockSpec(memory_space=pltpu.VMEM)
+    anywhere = pl.BlockSpec(memory_space=pl.ANY)
+    own, opp = pl.pallas_call(
+        functools.partial(kernel, n, cap),
+        out_shape=(jax.ShapeDtypeStruct((1, rd), jnp.float32),) * 2,
+        in_specs=[anywhere, anywhere, vmem, vmem, vmem, vmem],
+        out_specs=(vmem, vmem),
+        scratch_shapes=[
+            pltpu.VMEM((2, rd, width), jnp.bfloat16),
+            pltpu.VMEM((2, width, hid), jnp.bfloat16),
+            pltpu.VMEM((2, 1, hid), jnp.float32),
+            pltpu.VMEM((2, 1, rd), jnp.int32),
+            pltpu.VMEM((3, hs, cap, width), jnp.bfloat16),
+            pltpu.VMEM((4, hs, cap, width), jnp.bfloat16),
+            pltpu.VMEM((rd, width), jnp.bfloat16),
+            pltpu.VMEM((4, 1, rd), jnp.float32),
+            pltpu.VMEM((2, n, 1, rd), jnp.float32),
+            pltpu.VMEM((2, 1, rd), jnp.float32),
+            pltpu.SemaphoreType.DMA((2,)),
+            pltpu.SemaphoreType.DMA((2, 5)),
+            pltpu.SemaphoreType.DMA((4, hs)),
+            pltpu.SemaphoreType.DMA((4, hs)),
+            pltpu.SemaphoreType.DMA((4, hs)),
+            pltpu.SemaphoreType.DMA((4, hs)),
+        ],
+        compiler_params=pltpu.CompilerParams(collective_id=0, has_side_effects=True),
+    )(
+        observations, weights[0], gains, heads,
+        pairing.reshape(1, rd), valid.reshape(1, rd),
+    )
+    return own.reshape(rd), opp.reshape(rd)
+
+
+def per_device(observations, weights, gains, heads, pairing, valid):
+    rd = observations.shape[0]
+    n = lax.axis_size("league")
+    cap = 2 * rd // n
+    fits = (
+        n % 8 == 0 and cap % 16 == 0 and rd == 128
+        and lax.axis_size("rep") == 4 and weights.shape[2] % TILE == 0
+    )
+    plan = kernel_plan if fits else gathered_plan
+    return plan(observations, weights, gains, heads, pairing, valid)
+
+
 def solution(mesh):
     return jax.shard_map(
         per_device,

time: 99.5 us -> 47.9 us (0.48)
  waiting for transfers between devices: 47.7 us -> 0 us
  Pallas kernels: 0 us -> 44.8 us
  between operations: 14.1 us -> 0.64 us
  starting transfers between devices: 13 us -> 0 us
  matrix products: 11.6 us -> 0 us
  blocking collectives: 5.19 us -> 0 us
  local copies, waits for them, and re-layouts: 5.6 us -> 2.25 us
  other arithmetic: 2.02 us -> 0 us
    pallas_call x0 -> x1, Pallas kernels: none -> 44.8 us  [kernel_plan(): pl.pallas_call(functools.partial(kernel, n, cap), out_shape=(jax.ShapeDty...]
    all_gather x1 -> x0, waiting for transfers between devices: 25.6 us -> none  [per_device(): lax.all_gather(weight_cols, 'rep', axis=1, tiled=True)]
    all_to_all x2 -> x0, waiting for transfers between devices: 21.4 us -> none  [the longest x1 20.3 us: per_device(): lax.all_to_all(outgoing, 'league', split_axis=0, concat_axis=0, tiled=True)]
    all_to_all x2 -> x0, starting transfers between devices: 13 us -> none  [the longest x1 7.44 us: per_device(): lax.all_to_all(outgoing, 'league', split_axis=0, concat_axis=0, tiled=True)]
    dot_general x3 -> x0, matrix products: 11.6 us -> none  [the longest x2 11.4 us: normed_values(): jnp.dot(scaled, weight_cols, preferred_element_type=jnp.float32)]
    all_gather x1 -> x0, blocking collectives: 5.19 us -> none  [per_device(): lax.all_gather(head_cols, 'rep', axis=0, tiled=True)]
    unnamed x10 -> x2, local copies, waits for them, and re-layouts: 0.13 us -> 2.25 us
    scatter x1 -> x0, local copies, waits for them, and re-layouts: 1.72 us -> none  [per_device(): outgoing = jnp.zeros((n_league * capacity + 1, feature_width), jnp.bfloat...]
  transfers between devices with their start and end apart: 3 -> 0, of which waited for: 3 -> 0; matrix products, arithmetic and copies ran while one was open for 9% -> 0% of each run, Pallas kernels for 0% -> 0%
where the time goes in v1:
time: 47.9 us; the launch traced here: 47.7 us
  Pallas kernels  44.8 us (94%)
  local copies, waits for them, and re-layouts  2.25 us (5%)
  between operations  0.64 us (1%)
    pallas_call x1, Pallas kernels, kernel_plan(): pl.pallas_call(functools.partial(kernel, n, cap), out_shape=(jax.ShapeDty...  44.8 us
    unnamed x2, local copies, waits for them, and re-layouts  2.25 us

profile of v1, /device:TPU:0, one launch (start us, length us, event | category | flops | bytes accessed | tf_op | source)
XLA Modules:
  0.0 47.7 jit_solution(13544678930652723310)
XLA Ops:
  0.6 44.8 %shard_map.77 = (f32[1,128]{1,0:T(1,128)}, f32[1,128]{1,0:T(1,128)}) custom-call(bf16[128,2048]{1,0:T(8,128)(2,1)} %obs_hbm.1, bf16[2048,512]{1,0:T(8,128)(2,1)} %bitcast.5, f32[1,2048]{1,0:T(1,128)} %gain_ref.1, bf16[1,512]{1,0:T(2,128)(2,1)} %head_ref.1, s32[1,128]{1,0:T(1,128)} %bitcast.6, s32[1,128]{1,0:T(1,128)} %bitcast.7), custom_call_target="tpu_custom_call" | custom-call | tf_op jit(solution)/shard_map/pallas_call | solution.py:240
  45.5 1.1 %copy.10 = f32[128]{0:T(128)} copy(f32[128]{0:T(128)} %bitcast.9) | data formatting | bytes 1024
  46.6 1.1 %copy.11 = f32[128]{0:T(128)} copy(f32[128]{0:T(128)} %bitcast.8) | data formatting | bytes 1024

commit v2 on v1

--- a/solution.py
+++ b/solution.py
@@ -8,7 +8,8 @@
 from jax.sharding import PartitionSpec as P
 
 MESH = pl.DeviceIdType.MESH
-TILE = 256
+TILE = 512
+PARTS = 4
 
 
 def normed_values(obs_rows, agent_gain, weight_cols, head_cols):
@@ -56,9 +57,9 @@
 def kernel(
     n, cap,
     obs_hbm, w_hbm, gain_ref, head_ref, pair_ref, valid_ref,
-    own_ref, opp_ref,
+    out_ref,
     rows, wbuf, hv, code, slots, taken, scaled, res, back, vown,
-    lsem, asem, slot_send, slot_recv, back_send, back_recv,
+    lsem, asem, slot_send, slot_recv, far_send, far_recv, back_send, back_recv,
 ):
     hs = n // 2
     rd, width = rows.shape[1], rows.shape[2]
@@ -125,9 +126,6 @@
     def ahead(k):
         return lax.rem(pos + k, hs)
 
-    def behind(k):
-        return lax.rem(pos + hs - k, hs)
-
     send_code = remote(code.at[0], code.at[1], asem.at[0, 0], asem.at[1, 0], (lg, partner))
     send_rows = remote(rows.at[0], rows.at[1], asem.at[0, 1], asem.at[1, 1], (lg, partner))
     send_head = remote(hv.at[0], hv.at[1], asem.at[0, 2], asem.at[1, 2], (lg, sibling))
@@ -135,20 +133,50 @@
     send_code.start()
     send_rows.start()
 
-    def slot_copy(kind, k):
-        if kind == 3:
-            src, dst, to = taken.at[1, behind(k)], taken.at[3, behind(k)], (lg, partner)
-        else:
-            side = far_half if kind == 1 else half
-            src, dst, to = slots.at[kind, ahead(k)], taken.at[kind, pos], (side * hs + ahead(k), rp)
-        return remote(src, dst, slot_send.at[kind, k], slot_recv.at[kind, k], to)
-
-    first = {0: 1, 1: 0, 2: 1, 3: 0}
-    moves = {(kind, k): slot_copy(kind, k) for kind in range(4) for k in range(first[kind], hs)}
-    for k in range(hs):
-        moves[1, k].start()
+    def far_target(j):
+        return lax.rem(pos // 2 + 1 + j, 2) * 2 + lax.rem(pos + 1 + j // 2, 2)
+
+    def far_source(j):
+        return lax.rem(pos // 2 + 1 + j, 2) * 2 + lax.rem(pos + 1 + j // 2, 2)
+
+    def cut(ref, part):
+        span = width // PARTS
+        return ref.at[:, pl.ds(part * span, span)]
+
+    def far_copy(j, part):
+        to = far_target(j)
+        return remote(
+            cut(slots.at[1, to], part), cut(taken.at[1, pos], part),
+            far_send.at[0, to, part], far_recv.at[0, pos, part], (far_half * hs + to, rp),
+        )
+
+    def arrival(j, part):
+        q = far_source(j)
+        return remote(
+            cut(slots.at[1, q], part), cut(taken.at[1, q], part),
+            far_send.at[0, q, part], far_recv.at[0, q, part], (far_half * hs + q, rp),
+        )
+
+    def forward_copy(j, part):
+        q = far_source(j)
+        return remote(
+            cut(taken.at[1, q], part), cut(taken.at[3, q], part),
+            far_send.at[1, q, part], far_recv.at[1, q, part], (lg, partner),
+        )
+
+    def near_copy(kind, k):
+        return remote(
+            slots.at[kind, ahead(k)], taken.at[kind, pos],
+            slot_send.at[kind // 2, k], slot_recv.at[kind // 2, k], (half * hs + ahead(k), rp),
+        )
+
+    near = {(kind, k): near_copy(kind, k) for kind in (0, 2) for k in range(1, hs)}
+    far = [far_copy(j, part) for j in range(hs) for part in range(PARTS)]
+    onward = [forward_copy(j, part) for j in range(hs) for part in range(PARTS)]
+    for move in far:
+        move.start()
     for k in range(1, hs):
-        moves[0, k].start()
+        near[0, k].start()
     copy_w.wait()
     send_head.start()
     send_w.start()
@@ -171,6 +199,7 @@
         acc = lax.fori_loop(0, 2 * per, tile, jnp.zeros((rd, rd), jnp.float32))
         return jnp.sum(acc.T, axis=0, keepdims=True)
 
+    first = {0: 1, 1: 0, 2: 1, 3: 0}
     replies = {}
 
     def answer(kind):
@@ -194,28 +223,34 @@
     other_code = code[1]
     fill(2, 1, other_code, placing(other_code)[1], half)
     for k in range(1, hs):
-        moves[2, k].start()
-
-    def forward(k):
-        moves[1, k].wait_recv()
-        moves[3, k].start()
-
-    for k in range(hs // 2):
-        forward(k)
+        near[2, k].start()
+
+    def forward(j):
+        for part in range(PARTS):
+            arrival(j, part).wait_recv()
+            onward[j * PARTS + part].start()
+
+    forward(0)
     vown[0] = values(rows[1])
     send_own = remote(vown.at[0], vown.at[1], asem.at[0, 4], asem.at[1, 4], (lg, partner))
     send_own.start()
-    for k in range(hs // 2, hs):
-        forward(k)
-    for kind in (0, 1, 2, 3):
-        if kind != 1:
-            for k in range(first[kind], hs):
-                moves[kind, k].wait_recv()
-        answer(kind)
+    forward(1)
+    for k in range(1, hs):
+        near[0, k].wait_recv()
+    answer(0)
+    forward(2)
+    forward(3)
+    for k in range(1, hs):
+        near[2, k].wait_recv()
+    answer(2)
+    answer(1)
+    for move in onward:
+        move.wait_recv()
+    answer(3)
 
     send_own.wait_recv()
     own = mine + vown[1]
-    own_ref[...] = own
+    out_ref[0] = own
     for move in replies.values():
         move.wait_recv()
     table = jnp.concatenate([back[0, a] + back[1, a] for a in range(n)], axis=0)
@@ -224,8 +259,8 @@
     chosen = jnp.where(sub == my_slot + pos * cap, 1.0, 0.0)
     found = jnp.dot(table, chosen, preferred_element_type=jnp.float32, precision=lax.Precision.HIGHEST)
     opp = jnp.sum(jnp.where(my_pick > 0.0, found, 0.0), axis=0, keepdims=True)
-    opp_ref[...] = jnp.where(my_code == lg, own, opp)
-    for move in [send_code, send_rows, send_head, send_w, send_own, *moves.values(), *replies.values()]:
+    out_ref[1] = jnp.where(my_code == lg, own, opp)
+    for move in [send_code, send_rows, send_head, send_w, send_own, *near.values(), *far, *onward, *replies.values()]:
         move.wait_send()
 
 
@@ -237,11 +272,11 @@
     hs = n // 2
     vmem = pl.BlockSpec(memory_space=pltpu.VMEM)
     anywhere = pl.BlockSpec(memory_space=pl.ANY)
-    own, opp = pl.pallas_call(
+    both = pl.pallas_call(
         functools.partial(kernel, n, cap),
-        out_shape=(jax.ShapeDtypeStruct((1, rd), jnp.float32),) * 2,
+        out_shape=jax.ShapeDtypeStruct((2, 1, rd), jnp.float32),
         in_specs=[anywhere, anywhere, vmem, vmem, vmem, vmem],
-        out_specs=(vmem, vmem),
+        out_specs=vmem,
         scratch_shapes=[
             pltpu.VMEM((2, rd, width), jnp.bfloat16),
             pltpu.VMEM((2, width, hid), jnp.bfloat16),
@@ -255,8 +290,10 @@
             pltpu.VMEM((2, 1, rd), jnp.float32),
             pltpu.SemaphoreType.DMA((2,)),
             pltpu.SemaphoreType.DMA((2, 5)),
-            pltpu.SemaphoreType.DMA((4, hs)),
-            pltpu.SemaphoreType.DMA((4, hs)),
+            pltpu.SemaphoreType.DMA((2, hs)),
+            pltpu.SemaphoreType.DMA((2, hs)),
+            pltpu.SemaphoreType.DMA((2, hs, PARTS)),
+            pltpu.SemaphoreType.DMA((2, hs, PARTS)),
             pltpu.SemaphoreType.DMA((4, hs)),
             pltpu.SemaphoreType.DMA((4, hs)),
         ],
@@ -265,7 +302,7 @@
         observations, weights[0], gains, heads,
         pairing.reshape(1, rd), valid.reshape(1, rd),
     )
-    return own.reshape(rd), opp.reshape(rd)
+    return both[0, 0], both[1, 0]
 
 
 def per_device(observations, weights, gains, heads, pairing, valid):
@@ -273,7 +310,7 @@
     n = lax.axis_size("league")
     cap = 2 * rd // n
     fits = (
-        n % 8 == 0 and cap % 16 == 0 and rd == 128
+        n == 8 and cap % 16 == 0 and rd == 128
         and lax.axis_size("rep") == 4 and weights.shape[2] % TILE == 0
     )
     plan = kernel_plan if fits else gathered_plan

time: 47.9 us -> 44.9 us (0.937)
  Pallas kernels: 44.8 us -> 42.9 us
  local copies, waits for them, and re-layouts: 2.25 us -> 1.18 us
    unnamed x2 -> x0, local copies, waits for them, and re-layouts: 2.25 us -> none
    pallas_call x1, Pallas kernels: 44.8 us -> 42.9 us  [kernel_plan(): pl.pallas_call(functools.partial(kernel, n, cap), out_shape=jax.ShapeDtyp...]
    squeeze x0 -> x1, local copies, waits for them, and re-layouts: none -> 1.18 us  [kernel_plan(): return (both[0, 0], both[1, 0])]
where the time goes in v2:
time: 44.9 us; the launch traced here: 44.7 us
  Pallas kernels  42.9 us (96%)
  local copies, waits for them, and re-layouts  1.18 us (3%)
  between operations  0.64 us (1%)
    pallas_call x1, Pallas kernels, kernel_plan(): pl.pallas_call(functools.partial(kernel, n, cap), out_shape=jax.ShapeDtyp...  42.9 us
    squeeze x1, local copies, waits for them, and re-layouts, kernel_plan(): return (both[0, 0], both[1, 0])  1.18 us

profile of v2, /device:TPU:0, one launch (start us, length us, event | category | flops | bytes accessed | tf_op | source)
XLA Modules:
  0.0 44.7 jit_solution(4920536054068523269)
XLA Ops:
  0.6 42.9 %shard_map.77 = f32[2,1,128]{2,1,0:T(1,128)} custom-call(bf16[128,2048]{1,0:T(8,128)(2,1)} %obs_hbm.1, bf16[2048,512]{1,0:T(8,128)(2,1)} %bitcast.7, f32[1,2048]{1,0:T(1,128)} %gain_ref.1, bf16[1,512]{1,0:T(2,128)(2,1)} %head_ref.1, s32[1,128]{1,0:T(1,128)} %bitcast.8, s32[1,128]{1,0:T(1,128)} %bitcast.9), custom_call_target="tpu_custom_call" | custom-call | tf_op jit(solution)/shard_map/pallas_call | solution.py:275
  43.5 1.2 %slice_bitcast_fusion = (f32[128]{0:T(128)}, f32[128]{0:T(128)}) fusion(f32[2,1,128]{2,1,0:T(1,128)} %shard_map.77), kind=kLoop, calls=%fused_computation | loop fusion | bytes 2048 | tf_op jit(solution)/shard_map/squeeze | solution.py:305
